TPU v7x, 32 devices: a whole 2x2x4 slice. The times are simulated.
32 devices in a mesh: dp: 4 (over y, x), group: 8 (over z, core).
Axes of the slice: x: 2, y: 2, z: 4, core: 2. Of those that a mesh axis runs over, the one named last changes fastest.
Arguments:
- tokens: bfloat16 [2048, 5120], P('dp'), may hold values from -6 to 6
- frame_mask: int32 [2048], P('dp'), may hold values 0 or 1
- cotangent: bfloat16 [2048, 5120], P('dp'), may hold values from -0.625 to 0.625
- up_weight: bfloat16 [5120, 8192], P('dp', 'group'), may hold values from -0.078125 to 0.078125
- down_weight: bfloat16 [5120, 8192], P('dp', 'group'), may hold values from -0.0625 to 0.0625
- snap_params: bfloat16 [8, 32768], P(None, ('dp', 'group')), may hold values from -6 to 6
- first_moment: float32 [8, 32768], P(None, ('dp', 'group')), may hold values from -6 to 6
- second_moment: float32 [8, 32768], P(None, ('dp', 'group')), may hold values from 0.01 to 4
- range_of_writer: int32 [8], replicated, may hold values from 0 to 7, each once
Outputs:
- grad_up: float32 [5120, 8192], P('dp', 'group')
- grad_down: float32 [5120, 8192], P('dp', 'group')
- written_params: bfloat16 [8, 32768], P('group', 'dp')
- written_moments: float32 [2, 8, 32768], P(None, 'group', 'dp')
Inputs may be any that keep to these rules, and one draw needn't show every extreme that they name: `range_of_writer`: each of the 8 ranges is named by exactly one owner.
All inputs are finite; a program needn't handle non-finite values. No bound on the sum of `frame_mask` on one device may be relied on, other than what follows from the above.
Results may differ from a plain program's by a relative error of at most 0.017.
Values may be sent and summed in bfloat16 or wider, within the bound.
No kernel may reach another device: no remote copies, remote signals or barrier semaphores. Data moves between devices by JAX's collectives and lax.ppermute only.
A program may use at most 128 MiB of HBM per device.

v0:
```python
import jax
import jax.numpy as jnp
from jax import lax
from jax.sharding import PartitionSpec as P

EPS = 1e-06


def normalize(tokens):
    values = tokens.astype(jnp.float32)
    centred = values - jnp.mean(values, axis=1, keepdims=True)
    spread = jnp.mean(centred * centred, axis=1, keepdims=True)
    return (centred * lax.rsqrt(spread + EPS)).astype(jnp.bfloat16)


def gelu_pair(pre, d_act):
    act, pullback = jax.vjp(lambda v: jax.nn.gelu(v, approximate=True), pre)
    return (act.astype(jnp.bfloat16), pullback(d_act)[0].astype(jnp.bfloat16))


def outer_sum(left, right):
    return lax.dot_general(
        left, right, (((0,), (0,)), ((), ())), preferred_element_type=jnp.float32
    )


def regroup(snap_params, first_moment, second_moment, range_of_writer):
    send_params = jnp.take(snap_params, range_of_writer, axis=0)
    send_first = jnp.take(first_moment, range_of_writer, axis=0)
    send_second = jnp.take(second_moment, range_of_writer, axis=0)
    written_params = lax.all_to_all(send_params, "group", split_axis=0, concat_axis=1, tiled=True)
    got_first, got_second = (
        lax.all_to_all(
            send_first.astype(jnp.bfloat16), "group", split_axis=0, concat_axis=1, tiled=True
        ).astype(send_first.dtype),
        lax.all_to_all(
            send_second.astype(jnp.bfloat16), "group", split_axis=0, concat_axis=1, tiled=True
        ).astype(send_second.dtype),
    )
    return (written_params, jnp.stack([got_first, got_second]))


def per_device(
    tokens,
    frame_mask,
    cotangent,
    up_weight,
    down_weight,
    snap_params,
    first_moment,
    second_moment,
    range_of_writer,
):
    written = regroup(snap_params, first_moment, second_moment, range_of_writer)
    normed = normalize(tokens)
    masked = cotangent * frame_mask[:, None].astype(jnp.bfloat16)
    hidden_cols = up_weight.shape[1]
    left = normed
    right = masked
    pre = jnp.dot(
        left,
        lax.all_gather(up_weight, "dp", axis=0, tiled=True),
        preferred_element_type=jnp.float32,
    )
    d_act = jnp.dot(
        right,
        lax.all_gather(down_weight, "dp", axis=0, tiled=True),
        preferred_element_type=jnp.float32,
    )
    act, grad_pre = gelu_pair(pre, d_act)
    left = normed
    right = masked
    summed = lax.psum_scatter(
        jnp.concatenate([outer_sum(left, grad_pre), outer_sum(right, act)], axis=1).astype(
            jnp.bfloat16
        ),
        "dp",
        scatter_dimension=0,
        tiled=True,
    ).astype(jnp.float32)
    grad_up = summed[:, :hidden_cols]
    grad_down = summed[:, hidden_cols:]
    return (grad_up, grad_down, written[0], written[1])


def solution(mesh):
    placed = (
        P("dp", None),
        P("dp"),
        P("dp", None),
        P("dp", "group"),
        P("dp", "group"),
        P(None, ("dp", "group")),
        P(None, ("dp", "group")),
        P(None, ("dp", "group")),
        P(),
    )
    return jax.shard_map(
        per_device,
        mesh=mesh,
        in_specs=placed,
        out_specs=(P("dp", "group"), P("dp", "group"), P("group", "dp"), P(None, "group", "dp")),
        check_vma=False,
    )
```

profile of v0, /device:TPU:0, one launch (start us, length us, event | category | flops | bytes accessed | tf_op | source)
XLA Modules:
  0.0 468.0 jit_solution(11517369713372826682)
XLA Ops:
  7.2 0.7 all-gather.5.cloned.1.call-update
  8.0 0.7 all-gather.3.cloned.1.call-update
  8.8 3.4 convert_reduce_fusion
  12.2 0.6 copy-done.1
  12.8 1.5 fusion.2
  14.3 103.2 %all-gather.5.cloned.1.call-done = bf16[5120,1024]{1,0:T(8,128)(2,1)} async-done(((bf16[1280,1024]{1,0:T(8,128)(2,1)}), bf16[5120,1024]{1,0:T(8,128)(2,1)}) %all-gather.5.cloned.1.call-update) | async-done | bytes 10485776 | tf_op jit(solution)/shard_map/all_gather | solution.py:62
  117.5 9.9 %fusion.29 = f32[512,1024]{1,0:T(8,128)S(1)} fusion(bf16[5120,1024]{1,0:T(8,128)(2,1)} %all-gather.5.cloned.1.call-done, bf16[512,5120]{1,0:T(8,128)(2,1)} %param.11, f32[512]{0:T(512)S(1)} %add_rsqrt_fusion, f32[512]{0:T(512)S(1)} %broadcast_multiply_fusion), kind=kOutput, calls=%fused_computation.46 | convolution fusion | flops 5379194880 | bytes 17829888 | tf_op jit(solution)/shard_map/dot_general | solution.py:60
  127.5 11.7 %convolution_convert_fusion = bf16[5120,1024]{0,1:T(8,128)(2,1)} fusion(bf16[512,5120]{1,0:T(8,128)(2,1)} %param.13, bf16[512]{0:T(512)(128)(2,1)S(1)} %convert_element_type.54, f32[512,1024]{1,0:T(8,128)S(1)} %fusion.29), kind=kOutput, calls=%fused_computation.10 | convolution fusion | flops 5381292032 | bytes 17826816 | tf_op jit(solution)/shard_map/dot_general | solution.py:22
  139.1 85.2 %all-gather.3.cloned.1.call-done = bf16[5120,1024]{1,0:T(8,128)(2,1)} async-done(((bf16[1280,1024]{1,0:T(8,128)(2,1)}), bf16[5120,1024]{1,0:T(8,128)(2,1)}) %all-gather.3.cloned.1.call-update) | async-done | bytes 10485776 | tf_op jit(solution)/shard_map/all_gather | solution.py:67
  224.3 11.9 %fusion.15 = bf16[512,1024]{1,0:T(8,128)(2,1)S(1)} fusion(f32[512,1024]{1,0:T(8,128)S(1)} %fusion.29, bf16[5120,1024]{1,0:T(8,128)(2,1)} %all-gather.3.cloned.1.call-done, bf16[512,5120]{1,0:T(8,128)(2,1)} %param.13, bf16[512]{0:T(512)(128)(2,1)S(1)} %convert_element_type.54), kind=kOutput, calls=%fused_computation.25 | convolution fusion | flops 5381816320 | bytes 18875392 | tf_op jit(solution)/shard_map/dot_general | solution.py:65
  236.2 9.0 %convolution_convert_fusion.1 = bf16[5120,1024]{0,1:T(8,128)(2,1)S(1)} fusion(bf16[512,1024]{1,0:T(8,128)(2,1)S(1)} %fusion.15, bf16[512,5120]{1,0:T(8,128)(2,1)} %param.11, f32[512]{0:T(512)S(1)} %add_rsqrt_fusion, f32[512]{0:T(512)S(1)} %broadcast_multiply_fusion), kind=kOutput, calls=%fused_computation.11 | convolution fusion | flops 5384437760 | bytes 16781312 | tf_op jit(solution)/shard_map/dot_general | solution.py:22
  245.3 9.1 %pad_maximum_fusion = bf16[5120,2048]{0,1:T(8,128)(2,1)} fusion(bf16[5120,1024]{0,1:T(8,128)(2,1)S(1)} %bitcast.13, bf16[5120,1024]{0,1:T(8,128)(2,1)S(1)} %convolution_convert_fusion.1), kind=kLoop, calls=%fused_computation.3 | loop fusion | flops 41943040 | bytes 41943040 | tf_op jit(solution)/shard_map/concatenate | solution.py:74
  254.4 0.6 copy-done.5
  256.8 0.7 reduce.2
  257.5 0.6 reshape.139
  258.1 4.6 all-to-all-start.1
  262.7 0.7 reduce.1
  263.3 0.6 reshape.137
  264.0 0.6 gather_fusion
  264.5 3.8 all-to-all-done.1
  268.3 3.3 all-to-all-start.2
  271.8 0.7 reduce
  272.4 0.6 reshape.135
  273.1 4.2 all-to-all-done.2
  277.3 3.3 all-to-all-start
  280.7 5.5 %all-to-all-done = bf16[8,2,512]{2,1,0:T(2,128)(2,1)S(1)} async-done(((bf16[8,2,512]{2,1,0:T(2,128)(2,1)}), bf16[8,2,512]{2,1,0:T(2,128)(2,1)S(1)}, u32[]{:S(2)}, u32[]{:S(2)}) %all-to-all-start) | async-done | bytes 16416 | tf_op jit(solution)/shard_map/all_to_all | solution.py:31
  286.2 0.6 reshape.136
  286.8 0.7 maximum_convert_fusion
  287.6 154.8 %reduce-scatter.2.cloned.1.call-done = bf16[1280,2048]{0,1:T(8,128)(2,1)} async-done(((bf16[5120,2048]{0,1:T(8,128)(2,1)}), bf16[1280,2048]{0,1:T(8,128)(2,1)}) %reduce-scatter.2.cloned.1.call-update) | async-done | bytes 5242896 | tf_op jit(solution)/shard_map/reduce_scatter | solution.py:73
  442.3 7.4 %fusion.31 = (f32[1280,1024]{0,1:T(8,128)}, f32[1280,1024]{0,1:T(8,128)}) fusion(bf16[1280,2048]{0,1:T(8,128)(2,1)} %reduce-scatter.2.cloned.1.call-done), kind=kLoop, calls=%fused_computation.47 | loop fusion | bytes 20971520 | tf_op jit(solution)/shard_map/slice | solution.py:82
  449.7 5.9 %copy.18 = f32[1280,1024]{1,0:T(8,128)} copy(f32[1280,1024]{0,1:T(8,128)} %get-tuple-element.14) | data formatting | bytes 10485760
  455.6 5.9 %copy.19 = f32[1280,1024]{1,0:T(8,128)} copy(f32[1280,1024]{0,1:T(8,128)} %get-tuple-element.13) | data formatting | bytes 10485760
  (34 shorter events, 2.0 us)
Async XLA Ops:
  7.2 247.9 %copy-start = (f32[8,1024]{1,0:T(8,128)S(1)}, f32[8,1024]{1,0:T(8,128)}, u32[]{:S(2)}) copy-start(f32[8,1024]{1,0:T(8,128)} %param.17) | copy-start | bytes 98308
  7.2 1.5 copy-start.4
  7.2 110.3 %all-gather.5.cloned.1.call-start = ((), (), s32[]{:S(2)}) async-start(), calls=%async_computation.5 | async-start | bytes 13107200 | tf_op jit(solution)/shard_map/all_gather | solution.py:62
  7.9 216.4 %all-gather.3.cloned.1.call-start = ((), (), s32[]{:S(2)}) async-start(), calls=%async_computation.4 | async-start | bytes 13107200 | tf_op jit(solution)/shard_map/all_gather | solution.py:67
  8.7 433.6 %reduce-scatter.2.cloned.1.call-start = ((), (), s32[]{:S(2)}) async-start(), calls=%async_computation.6 | async-start | bytes 26214400 | tf_op jit(solution)/shard_map/reduce_scatter | solution.py:73
  8.7 4.0 copy-start.1
  224.3 20.9 %slice-start = ((s8[10485760]{0:T(1024)(128)(4,1)}), s8[4194304]{0:T(1024)(128)(4,1)S(1)}, s32[]{:S(2)}) async-start(s8[10485760]{0:T(1024)(128)(4,1)} %bitcast.12), calls=%async_computation.7 | async-start | bytes 8388608
  224.3 20.9 %slice-start.1 = ((s8[10485760]{0:T(1024)(128)(4,1)}), s8[4194304]{0:T(1024)(128)(4,1)S(1)}, s32[]{:S(2)}) async-start(s8[10485760]{0:T(1024)(128)(4,1)} %bitcast.12), calls=%async_computation.8 | async-start | bytes 8388608
  236.2 9.0 %slice-start.2 = ((s8[10485760]{0:T(1024)(128)(4,1)}), s8[2097152]{0:T(1024)(128)(4,1)S(1)}, s32[]{:S(2)}) async-start(s8[10485760]{0:T(1024)(128)(4,1)} %bitcast.12), calls=%async_computation.9 | async-start | bytes 4194304
  254.4 0.7 copy-start.5
  254.4 1.2 copy-start.3
  254.4 9.6 %copy-start.2 = (bf16[8,1024]{1,0:T(8,128)(2,1)S(1)}, bf16[8,1024]{1,0:T(8,128)(2,1)}, u32[]{:S(2)}) copy-start(bf16[8,1024]{1,0:T(8,128)(2,1)} %param.16) | copy-start | bytes 49156
  258.1 10.3 %all-to-all-start.1 = ((bf16[8,2,512]{2,1,0:T(2,128)(2,1)}), bf16[8,2,512]{2,1,0:T(2,128)(2,1)S(1)}, u32[]{:S(2)}, u32[]{:S(2)}) async-start(bf16[8,2,512]{2,1,0:T(2,128)(2,1)} %reshape.139), calls=%async_computation.2 | async-start | bytes 32768 | tf_op jit(solution)/shard_map/all_to_all | solution.py:33
  268.3 8.9 %all-to-all-start.2 = ((bf16[8,2,512]{2,1,0:T(2,128)(2,1)}), bf16[8,2,512]{2,1,0:T(2,128)(2,1)S(1)}, u32[]{:S(2)}, u32[]{:S(2)}) async-start(bf16[8,2,512]{2,1,0:T(2,128)(2,1)} %reshape.137), calls=%async_computation.3 | async-start | bytes 32768 | tf_op jit(solution)/shard_map/all_to_all | solution.py:36
  277.3 8.9 %all-to-all-start = ((bf16[8,2,512]{2,1,0:T(2,128)(2,1)}), bf16[8,2,512]{2,1,0:T(2,128)(2,1)S(1)}, u32[]{:S(2)}, u32[]{:S(2)}) async-start(bf16[8,2,512]{2,1,0:T(2,128)(2,1)} %reshape.135), calls=%async_computation.1 | async-start | bytes 32768 | tf_op jit(solution)/shard_map/all_to_all | solution.py:31
Sparse Core Ops, SparseCore 0:
  9.8 107.6 all-gather.4
  119.4 104.9 all-gather.2
  254.5 187.7 reduce-scatter.1
where the time goes:
time: 469 us; the launch traced here: 468 us
  waiting for transfers between devices  358 us (76%)
  matrix products  42.5 us (9%)
  local copies, waits for them, and re-layouts  25.2 us (5%)
  other arithmetic  16.9 us (4%)
  between operations  13.9 us (3%)
  starting transfers between devices  11.4 us (2%)
    reduce_scatter x1, waiting for transfers between devices, per_device(): lax.psum_scatter(jnp.concatenate([outer_sum(left, grad_pre), outer_sum(ri...  155 us
    all_gather x1, waiting for transfers between devices, per_device(): lax.all_gather(up_weight, 'dp', axis=0, tiled=True)  103 us
    all_gather x1, waiting for transfers between devices, per_device(): lax.all_gather(down_weight, 'dp', axis=0, tiled=True)  85.2 us
    dot_general x2, matrix products, outer_sum(): lax.dot_general(left, right, (((0,), (0,)), ((), ())), preferred_element_...  20.7 us
    unnamed x26, local copies, waits for them, and re-layouts  15.6 us
    dot_general x1, matrix products, per_device(): jnp.dot(right, lax.all_gather(down_weight, 'dp', axis=0, tiled=True), pre...  11.9 us
    dot_general x1, matrix products, per_device(): jnp.dot(left, lax.all_gather(up_weight, 'dp', axis=0, tiled=True), prefer...  9.93 us
  transfers between devices with their start and end apart: 6, of which 6 were waited for; matrix products, arithmetic and copies ran while one was open for 7% of the time, Pallas kernels for 0%

commit v1 on v0

--- a/solution.py
+++ b/solution.py
@@ -1,9 +1,43 @@
+import functools
 import jax
 import jax.numpy as jnp
 from jax import lax
 from jax.sharding import PartitionSpec as P
+from jax.lax import axis_index, axis_size, ppermute
 
 EPS = 1e-06
+
+
+def change_units(local_x, where_dim):
+    local_x = jnp.moveaxis(local_x, 0, where_dim)
+    long_array = local_x.shape
+    return local_x.reshape(
+        *long_array[:where_dim],
+        long_array[where_dim] * long_array[where_dim + 1],
+        *long_array[where_dim + 2 :]
+    )
+
+
+def work_the_stacks_all(row_data, which_axis, axis_k):
+    nodes = axis_size(which_axis)
+    inbox = [(ii, (ii + 1) % nodes) for ii in range(nodes)]
+    w_next, local_part = ([], [])
+    column = [(u, hop_no) for hop_no, u in inbox]
+    for ix in range(nodes - 1):
+        if ix % 2 == 0:
+            opened = ppermute(w_next[-1] if w_next else row_data, which_axis, inbox)
+            w_next.append(opened)
+        else:
+            local_part.append(
+                ppermute(local_part[-1] if local_part else row_data, which_axis, column)
+            )
+    kept_arr = jnp.stack([*w_next[::-1], row_data, *local_part])
+    item_now = axis_index(which_axis) - len(w_next)
+    kept_arr = kept_arr[(jnp.arange(nodes) - item_now) % nodes]
+    return change_units(kept_arr, axis_k)
+
+
+_read_slots = functools.partial(work_the_stacks_all, which_axis="dp", axis_k=0)
 
 
 def normalize(tokens):
@@ -62,11 +96,7 @@
         lax.all_gather(up_weight, "dp", axis=0, tiled=True),
         preferred_element_type=jnp.float32,
     )
-    d_act = jnp.dot(
-        right,
-        lax.all_gather(down_weight, "dp", axis=0, tiled=True),
-        preferred_element_type=jnp.float32,
-    )
+    d_act = jnp.dot(right, _read_slots(down_weight), preferred_element_type=jnp.float32)
     act, grad_pre = gelu_pair(pre, d_act)
     left = normed
     right = masked

time: 469 us -> 574 us (1.22)
  waiting for transfers between devices: 358 us -> 414 us
  other arithmetic: 16.9 us -> 40.4 us
  local copies, waits for them, and re-layouts: 25.2 us -> 46 us
  starting transfers between devices: 11.4 us -> 18.2 us
    ppermute x0 -> x3, waiting for transfers between devices: none -> 245 us  [the longest x2 149 us: work_the_stacks_all(): opened = ppermute(w_next[-1] if w_next else row_data, which_axis, inbox)]
    all_gather x1, waiting for transfers between devices: 103 us -> 0.01 us  [per_device(): lax.all_gather(up_weight, 'dp', axis=0, tiled=True)]
    all_gather x1 -> x0, waiting for transfers between devices: 85.2 us -> none  [per_device(): lax.all_gather(down_weight, 'dp', axis=0, tiled=True)]
    gather x0 -> x3, local copies, waits for them, and re-layouts: none -> 20.8 us  [work_the_stacks_all(): kept_arr = kept_arr[(jnp.arange(nodes) - item_now) % nodes]]
    unnamed x1 -> x2, other arithmetic: 0.01 us -> 11.8 us
    another operation x0 -> x1, other arithmetic: none -> 7.32 us  [work_the_stacks_all(): kept_arr = jnp.stack([*w_next[::-1], row_data, *local_part])]
    ppermute x0 -> x3, starting transfers between devices: none -> 6.42 us  [the longest x2 5.39 us: work_the_stacks_all(): opened = ppermute(w_next[-1] if w_next else row_data, which_axis, inbox)]
    unnamed x26 -> x24, local copies, waits for them, and re-layouts: 15.6 us -> 15.5 us
  transfers between devices with their start and end apart: 6 -> 8, of which waited for: 6 -> 7; matrix products, arithmetic and copies ran while one was open for 7% -> 9% of each run, Pallas kernels for 0% -> 0%
where the time goes in v1:
time: 574 us; the launch traced here: 572 us
  waiting for transfers between devices  414 us (72%)
  local copies, waits for them, and re-layouts  46 us (8%)
  other arithmetic  40.4 us (7%)
  matrix products  39.4 us (7%)
  starting transfers between devices  18.2 us (3%)
  between operations  14.2 us (2%)
    reduce_scatter x1, waiting for transfers between devices, per_device(): lax.psum_scatter(jnp.concatenate([outer_sum(left, grad_pre), outer_sum(ri...  155 us
    ppermute x2, waiting for transfers between devices, work_the_stacks_all(): opened = ppermute(w_next[-1] if w_next else row_data, which_axis, inbox)  149 us
    ppermute x1, waiting for transfers between devices, work_the_stacks_all(): ppermute(local_part[-1] if local_part else row_data, which_axis, column)  95.8 us
    gather x3, local copies, waits for them, and re-layouts, work_the_stacks_all(): kept_arr = kept_arr[(jnp.arange(nodes) - item_now) % nodes]  20.8 us
    dot_general x2, matrix products, outer_sum(): lax.dot_general(left, right, (((0,), (0,)), ((), ())), preferred_element_...  17.4 us
    unnamed x24, local copies, waits for them, and re-layouts  15.5 us
    concatenate x1, other arithmetic, per_device(): jnp.concatenate([outer_sum(left, grad_pre), outer_sum(right, act)], axis=1)  12.8 us
    dot_general x1, matrix products, per_device(): jnp.dot(right, _read_slots(down_weight), preferred_element_type=jnp.float32)  12.1 us
  transfers between devices with their start and end apart: 8, of which 7 were waited for; matrix products, arithmetic and copies ran while one was open for 9% of the time, Pallas kernels for 0%

profile of v1, /device:TPU:0, one launch (start us, length us, event | category | flops | bytes accessed | tf_op | source)
XLA Modules:
  0.0 572.4 jit_solution(4507546150809714010)
XLA Ops:
  7.2 0.7 all-gather.2.cloned.1.call-update
  8.0 3.0 collective-permute-start
  11.0 1.0 collective-permute-start.2
  12.0 94.5 %collective-permute-done = bf16[1280,1024]{1,0:T(8,128)(2,1)S(1)} collective-permute-done((bf16[1280,1024]{1,0:T(8,128)(2,1)}, bf16[1280,1024]{1,0:T(8,128)(2,1)S(1)}, u32[]{:S(2)}, u32[]{:S(2)}) %collective-permute-start) | collective-permute-done | bytes 2621472 | tf_op jit(solution)/shard_map/ppermute | solution.py:28
  106.5 2.4 collective-permute-start.1
  108.9 0.7 convert_element_type.54
  109.6 3.4 convert_reduce_fusion
  113.6 1.5 fusion.2
  115.1 95.8 %collective-permute-done.2 = bf16[1280,1024]{1,0:T(8,128)(2,1)} collective-permute-done((bf16[1280,1024]{1,0:T(8,128)(2,1)}, bf16[1280,1024]{1,0:T(8,128)(2,1)}, u32[]{:S(2)}, u32[]{:S(2)}) %collective-permute-start.2) | collective-permute-done | bytes 2621472 | tf_op jit(solution)/shard_map/ppermute | solution.py:32
  210.9 54.8 %collective-permute-done.1 = bf16[1280,1024]{1,0:T(8,128)(2,1)} collective-permute-done((bf16[1280,1024]{1,0:T(8,128)(2,1)S(1)}, bf16[1280,1024]{1,0:T(8,128)(2,1)}, u32[]{:S(2)}, u32[]{:S(2)}) %collective-permute-start.1) | collective-permute-done | bytes 2621472 | tf_op jit(solution)/shard_map/ppermute | solution.py:28
  265.7 7.3 %pad_maximum_fusion.1 = bf16[4,1280,1024]{2,1,0:T(8,128)(2,1)} fusion(bf16[1,1280,1024]{2,1,0:T(8,128)(2,1)} %bitcast.3, bf16[1,1280,1024]{2,1,0:T(8,128)(2,1)S(1)} %bitcast.22, bf16[1,1280,1024]{2,1,0:T(8,128)(2,1)S(1)} %bitcast.23, bf16[1,1280,1024]{2,1,0:T(8,128)(2,1)} %bitcast), kind=kLoop, calls=%fused_computation.12 | loop fusion | flops 15728640 | bytes 20971520 | tf_op jit(solution)/shard_map/stack | solution.py:34
  273.1 9.4 %fusion.33 = (bf16[4,640,1024]{2,1,0:T(8,128)(2,1)}, bf16[4,640,1024]{2,1,0:T(8,128)(2,1)}) fusion(bf16[4,1280,1024]{2,1,0:T(8,128)(2,1)} %pad_maximum_fusion.1), kind=kLoop, calls=%fused_computation.58 | loop fusion | bytes 20971520 | tf_op jit(solution)/shard_map/gather | solution.py:36
  282.5 5.7 gather_fusion.1
  288.2 5.7 %gather_fusion.2 = bf16[4,640,1024]{2,1,0:T(8,128)(2,1)} fusion(bf16[4,640,1024]{2,1,0:T(8,128)(2,1)} %get-tuple-element.14, s32[1024]{0:T(1024)S(1)} %pad_clamp_fusion.1), kind=kCustom, calls=%fused_computation.4 | custom fusion | bytes 10485776 | tf_op jit(solution)/shard_map/gather | solution.py:36
  293.9 11.8 %pad_maximum_fusion.2 = bf16[4,1280,1024]{2,1,0:T(8,128)(2,1)} fusion(bf16[4,640,1024]{2,1,0:T(8,128)(2,1)} %gather_fusion.2, bf16[4,640,1024]{2,1,0:T(8,128)(2,1)} %gather_fusion.1), kind=kLoop, calls=%fused_computation.13 | loop fusion | flops 20971520 | bytes 20971520
  305.7 9.9 %fusion.31 = f32[512,1024]{1,0:T(8,128)S(1)} fusion(bf16[5120,1024]{1,0:T(8,128)(2,1)} %all-gather.2.cloned.1.call-done, bf16[512,5120]{1,0:T(8,128)(2,1)} %param.11, f32[512]{0:T(512)S(1)} %add_rsqrt_fusion, f32[512]{0:T(512)S(1)} %broadcast_multiply_fusion), kind=kOutput, calls=%fused_computation.57 | convolution fusion | flops 5379194880 | bytes 17829888 | tf_op jit(solution)/shard_map/dot_general | solution.py:94
  315.6 8.8 %convolution_convert_fusion = bf16[5120,1024]{0,1:T(8,128)(2,1)S(1)} fusion(bf16[512,5120]{1,0:T(8,128)(2,1)} %param.13, bf16[512]{0:T(512)(128)(2,1)S(1)} %convert_element_type.54, f32[512,1024]{1,0:T(8,128)S(1)} %fusion.31), kind=kOutput, calls=%fused_computation.14 | convolution fusion | flops 5381292032 | bytes 17826816 | tf_op jit(solution)/shard_map/dot_general | solution.py:56
  324.4 12.1 %fusion.15 = bf16[512,1024]{1,0:T(8,128)(2,1)S(1)} fusion(f32[512,1024]{1,0:T(8,128)S(1)} %fusion.31, bf16[5120,1024]{1,0:T(8,128)(2,1)} %bitcast.21, bf16[512,5120]{1,0:T(8,128)(2,1)} %param.13, bf16[512]{0:T(512)(128)(2,1)S(1)} %convert_element_type.54), kind=kOutput, calls=%fused_computation.29 | convolution fusion | flops 5381816320 | bytes 18875392 | tf_op jit(solution)/shard_map/dot_general | solution.py:99
  336.5 8.6 %convolution_convert_fusion.1 = bf16[5120,1024]{0,1:T(8,128)(2,1)} fusion(bf16[512,1024]{1,0:T(8,128)(2,1)S(1)} %fusion.15, bf16[512,5120]{1,0:T(8,128)(2,1)S(1)} %bitcast.20, f32[512]{0:T(512)S(1)} %add_rsqrt_fusion, f32[512]{0:T(512)S(1)} %broadcast_multiply_fusion), kind=kOutput, calls=%fused_computation.15 | convolution fusion | flops 5384437760 | bytes 16781312 | tf_op jit(solution)/shard_map/dot_general | solution.py:56
  345.1 12.8 %pad_maximum_fusion = bf16[5120,2048]{0,1:T(8,128)(2,1)} fusion(bf16[5120,1024]{0,1:T(8,128)(2,1)S(1)} %convolution_convert_fusion, bf16[5120,1024]{0,1:T(8,128)(2,1)} %convolution_convert_fusion.1), kind=kLoop, calls=%fused_computation.5 | loop fusion | flops 41943040 | bytes 41943040 | tf_op jit(solution)/shard_map/concatenate | solution.py:104
  361.6 5.1 all-to-all-start.2
  368.6 3.8 all-to-all-done.2
  372.4 3.3 all-to-all-start.1
  375.8 0.7 reduce
  377.1 4.2 all-to-all-done.1
  381.3 3.3 all-to-all-start
  384.7 5.5 all-to-all-done
  390.9 0.7 maximum_convert_fusion
  391.6 154.8 %reduce-scatter.2.cloned.1.call-done = bf16[1280,2048]{0,1:T(8,128)(2,1)} async-done(((bf16[5120,2048]{0,1:T(8,128)(2,1)}), bf16[1280,2048]{0,1:T(8,128)(2,1)}) %reduce-scatter.2.cloned.1.call-update) | async-done | bytes 5242896 | tf_op jit(solution)/shard_map/reduce_scatter | solution.py:103
  546.4 7.4 %fusion.34 = (f32[1280,1024]{0,1:T(8,128)}, f32[1280,1024]{0,1:T(8,128)}) fusion(bf16[1280,2048]{0,1:T(8,128)(2,1)} %reduce-scatter.2.cloned.1.call-done), kind=kLoop, calls=%fused_computation.59 | loop fusion | bytes 20971520 | tf_op jit(solution)/shard_map/slice | solution.py:112
  553.8 5.9 %copy.18 = f32[1280,1024]{1,0:T(8,128)} copy(f32[1280,1024]{0,1:T(8,128)} %get-tuple-element.16) | data formatting | bytes 10485760
  559.7 5.9 %copy.19 = f32[1280,1024]{1,0:T(8,128)} copy(f32[1280,1024]{0,1:T(8,128)} %get-tuple-element.15) | data formatting | bytes 10485760
  (42 shorter events, 7.6 us)
Async XLA Ops:
  7.2 351.4 %copy-start = (f32[8,1024]{1,0:T(8,128)S(1)}, f32[8,1024]{1,0:T(8,128)}, u32[]{:S(2)}) copy-start(f32[8,1024]{1,0:T(8,128)} %param.17) | copy-start | bytes 98308
  7.2 298.5 %all-gather.2.cloned.1.call-start = ((), (), s32[]{:S(2)}) async-start(), calls=%async_computation.4 | async-start | bytes 13107200 | tf_op jit(solution)/shard_map/all_gather | solution.py:96
  7.9 538.5 %reduce-scatter.2.cloned.1.call-start = ((), (), s32[]{:S(2)}) async-start(), calls=%async_computation.5 | async-start | bytes 26214400 | tf_op jit(solution)/shard_map/reduce_scatter | solution.py:103
  8.0 98.6 %collective-permute-start = (bf16[1280,1024]{1,0:T(8,128)(2,1)}, bf16[1280,1024]{1,0:T(8,128)(2,1)S(1)}, u32[]{:S(2)}, u32[]{:S(2)}) collective-permute-start(bf16[1280,1024]{1,0:T(8,128)(2,1)} %param.15), channel_id=1, source_target_pairs={{0,8},{8,16},{16,24},{24,0},{1,9},{9,17},{17,25},{25,1},{2,10},{10... | collective-permute-start | bytes 7864328 | tf_op jit(solution)/shard_map/ppermute | solution.py:28
  11.0 200.0 %collective-permute-start.2 = (bf16[1280,1024]{1,0:T(8,128)(2,1)}, bf16[1280,1024]{1,0:T(8,128)(2,1)}, u32[]{:S(2)}, u32[]{:S(2)}) collective-permute-start(bf16[1280,1024]{1,0:T(8,128)(2,1)} %param.15), channel_id=1, source_target_pairs={{8,0},{16,8},{24,16},{0,24},{9,1},{17,9},{25,17},{1,25},{10,2},{18... | collective-permute-start | bytes 7864328 | tf_op jit(solution)/shard_map/ppermute | solution.py:32
  106.5 159.2 %collective-permute-start.1 = (bf16[1280,1024]{1,0:T(8,128)(2,1)S(1)}, bf16[1280,1024]{1,0:T(8,128)(2,1)}, u32[]{:S(2)}, u32[]{:S(2)}) collective-permute-start(bf16[1280,1024]{1,0:T(8,128)(2,1)S(1)} %collective-permute-done), channel_id=1, source_target_pairs={{0,8},{8,16},{16,24},{24,0},{1,9},{9,17},{17,25},{25,1},{2,10},{10... | collective-permute-start | bytes 7864328 | tf_op jit(solution)/shard_map/ppermute | solution.py:28
  109.6 4.0 copy-start.1
  109.6 156.1 %copy-start.2 = (bf16[1280,1024]{1,0:T(8,128)(2,1)S(1)}, bf16[1280,1024]{1,0:T(8,128)(2,1)}, u32[]{:S(2)}) copy-start(bf16[1280,1024]{1,0:T(8,128)(2,1)} %param.15) | copy-start | bytes 7864324
  315.6 20.9 %slice-start = ((s8[5242880]{0:T(1024)(128)(4,1)}), s8[1048576]{0:T(1024)(128)(4,1)S(1)}, s32[]{:S(2)}) async-start(s8[5242880]{0:T(1024)(128)(4,1)} %bitcast.19), calls=%async_computation.6 | async-start | bytes 2097152
  324.4 12.1 %slice-start.1 = ((s8[5242880]{0:T(1024)(128)(4,1)}), s8[4194304]{0:T(1024)(128)(4,1)S(1)}, s32[]{:S(2)}) async-start(s8[5242880]{0:T(1024)(128)(4,1)} %bitcast.19), calls=%async_computation.7 | async-start | bytes 8388608
  357.9 0.7 copy-start.5
  357.9 1.2 copy-start.4
  357.9 10.1 %copy-start.3 = (bf16[8,1024]{1,0:T(8,128)(2,1)S(1)}, bf16[8,1024]{1,0:T(8,128)(2,1)}, u32[]{:S(2)}) copy-start(bf16[8,1024]{1,0:T(8,128)(2,1)} %param.16) | copy-start | bytes 49156
  361.6 10.7 %all-to-all-start.2 = ((bf16[8,2,512]{2,1,0:T(2,128)(2,1)}), bf16[8,2,512]{2,1,0:T(2,128)(2,1)S(1)}, u32[]{:S(2)}, u32[]{:S(2)}) async-start(bf16[8,2,512]{2,1,0:T(2,128)(2,1)} %reshape.206), calls=%async_computation.3 | async-start | bytes 32768 | tf_op jit(solution)/shard_map/all_to_all | solution.py:70
  372.4 8.9 %all-to-all-start.1 = ((bf16[8,2,512]{2,1,0:T(2,128)(2,1)}), bf16[8,2,512]{2,1,0:T(2,128)(2,1)S(1)}, u32[]{:S(2)}, u32[]{:S(2)}) async-start(bf16[8,2,512]{2,1,0:T(2,128)(2,1)} %reshape.208), calls=%async_computation.2 | async-start | bytes 32768 | tf_op jit(solution)/shard_map/all_to_all | solution.py:67
  381.3 8.9 %all-to-all-start = ((bf16[8,2,512]{2,1,0:T(2,128)(2,1)}), bf16[8,2,512]{2,1,0:T(2,128)(2,1)S(1)}, u32[]{:S(2)}, u32[]{:S(2)}) async-start(bf16[8,2,512]{2,1,0:T(2,128)(2,1)} %reshape.204), calls=%async_computation.1 | async-start | bytes 32768 | tf_op jit(solution)/shard_map/all_to_all | solution.py:65
Sparse Core Ops, SparseCore 0:
  9.8 191.6 all-gather.1
  358.1 188.2 reduce-scatter.1
